TPU v7x, 32 devices: a whole 2x2x4 slice. The times are simulated.
32 devices in a mesh: seq: 16 (over z, x, core), head: 2 (over y).
Axes of the slice: x: 2, y: 2, z: 4, core: 2. Of those that a mesh axis runs over, the one named last changes fastest.
Arguments:
- old_cache: bfloat16 [1024, 8, 128, 128], P(('seq', 'head')), may hold values from -9 to 9
- page_dest: int32 [1024], P(('seq', 'head')), may hold values from 0 to 1023, as said below
- seq_pages: int32 [32], replicated, may hold values from 1 to 64, 1024 in all
- last_fill: int32 [32], replicated, may hold values from 1 to 128
- queries: bfloat16 [32, 8, 512], P(None, 'head'), may hold values from -16 to 16
Outputs:
- new_cache: bfloat16 [1024, 8, 128, 128], P('seq', 'head')
- attended: bfloat16 [32, 8, 512], P('seq', 'head')
Inputs may be any that keep to these rules, and one draw needn't show every extreme that they name: page_dest is a permutation of the page numbers. The 64 old pages p with the same p // 64 go to exactly 16 distinct new owners page_dest[p] // 64, exactly 4 pages to each; every new owner receives 64 pages.
All inputs are finite; a program needn't handle non-finite values.
Results may differ from a plain program's by a relative error of at most 0.004.
Values may be sent and summed in bfloat16 or wider, within the bound.
No kernel may reach another device: no remote copies, remote signals or barrier semaphores. Data moves between devices by JAX's collectives and lax.ppermute only.
A program may use at most 64 MiB of HBM per device.

v0:
```python
import functools
import jax
import jax.numpy as jnp
from jax import lax
from jax.experimental import pallas as pl
from jax.experimental.pallas import tpu as pltpu
from jax.sharding import PartitionSpec as P

NEG_FILL = -1e30
LABEL_ROWS = 8
SHARES = (1, 2, 3, 4, 8, 8, 6)
KINDS = ("fwd", "fwd", "fwd", "fwd", "all", "far", "all")

HBM = pl.BlockSpec(memory_space=pltpu.HBM)
SMEM = pl.BlockSpec(memory_space=pltpu.SMEM)
VMEM = pl.BlockSpec(memory_space=pltpu.VMEM)


def partner(me, k, peers):
    if peers & (peers - 1) == 0:
        return me ^ k
    return (me + k) % peers


def sender(me, k, peers):
    if peers & (peers - 1) == 0:
        return me ^ k
    return (me + peers - k) % peers


class Geometry:
    def __init__(self, pages_own, groups, peers, rows):
        self.pages_own, self.groups, self.peers, self.rows = pages_own, groups, peers, rows
        self.page_count = pages_own * groups
        self.cap = self.page_count // min(peers, 16)
        self.full = peers * self.cap == self.page_count


def spread(pieces):
    offset, laid = 0, []
    for start, length in pieces:
        laid.append((start, length, offset))
        offset += length
    return laid, offset


def granted(*sizes):
    return pltpu.CompilerParams(vmem_limit_bytes=(4 << 20) + sum(sizes))


def estimate(moved):
    return pl.CostEstimate(flops=moved * 4, bytes_accessed=moved, transcendentals=0)


def pack_kernel(g, ks, single, pieces, passed, extra, label, *refs):
    laid, length = spread(pieces)
    dests, old, refs = refs[:g.groups], refs[g.groups], refs[g.groups + 1:]
    count = len(pieces) * (g.groups - 1)
    received, refs = refs[:count], refs[count:]
    head, me = lax.axis_index("head"), lax.axis_index("seq")
    forwarded, refs = refs[:len(passed)], refs[len(passed):]
    tail = None
    if extra and not label:
        tail, refs = refs[0], refs[1:]
    number = g.peers if ks is None else len(ks)
    if single:
        outs, refs = [refs[0].at[i] for i in range(number)], refs[1:]
    else:
        outs, refs = refs[:number], refs[number:]
    if ks is None:
        targets = list(range(g.peers))
    else:
        targets = [partner(me, k, g.peers) for k in ks]
    stage, counts, order, slot, in_sem, out_sem = refs[:6]
    pass_stages, refs = refs[6:6 + len(passed)], refs[6 + len(passed):]
    copies = []
    for c, (start, size, offset) in enumerate(laid):
        row = pl.multiple_of(head * g.rows + start, 8)
        copies.append(pltpu.make_async_copy(
            old.at[:, pl.ds(row, size), :],
            stage.at[pl.ds(0, g.pages_own), pl.ds(offset, size), :], in_sem.at[c]))
        for j in range(1, g.groups):
            i = (j - 1) * len(pieces) + c
            copies.append(pltpu.make_async_copy(
                received[i],
                stage.at[pl.ds(j * g.pages_own, g.pages_own), pl.ds(offset, size), :],
                in_sem.at[len(pieces) + i]))
    arrivals = []
    if passed:
        pass_in, pass_out = refs
        arrivals = [pltpu.make_async_copy(block, place, pass_in.at[c]) for c, (block, place)
                    in enumerate(zip(forwarded, pass_stages))]
    for copy in copies + arrivals:
        copy.start()

    @pl.loop(0, g.peers, unroll=8)
    def _(t):
        counts[t] = 0

    if not g.full:
        @pl.loop(0, g.peers * g.cap)
        def _(i):
            order[i] = -1

    for j, dest in enumerate(dests):
        @pl.loop(0, g.pages_own, unroll=8)
        def _(i):
            d = dest[i]
            if g.page_count & (g.page_count - 1) == 0:
                t = lax.shift_right_logical(d, g.page_count.bit_length() - 1)
            else:
                t = d // g.page_count
            n = counts[t]
            counts[t] = n + 1
            order[t * g.cap + n] = j * g.pages_own + i
            if label:
                slot[t * g.cap + n] = d - t * g.page_count

    for i, t in enumerate(targets):
        block = outs[i]
        if tail is not None:
            block[g.cap * length:, :] = tail[t]
        if label:
            lane = lax.broadcasted_iota(jnp.int32, (extra, 128), 1)
            tile = jnp.full((extra, 128), -1, jnp.int32)
            for n in range(g.cap):
                value = slot[t * g.cap + n]
                if not g.full:
                    value = jnp.where(order[t * g.cap + n] >= 0, value, -1)
                tile = jnp.where(lane == n, value, tile)
            block[g.cap * length:, :] = tile.astype(jnp.float32).astype(jnp.bfloat16)
    for copy in copies:
        copy.wait()
    if not passed:
        for i, t in enumerate(targets):
            for n in range(g.cap):
                p = order[t * g.cap + n]
                outs[i][n * length:(n + 1) * length, :] = stage[p if g.full else jnp.maximum(p, 0)]
        return

    def page_copy(i, n, p):
        return pltpu.make_async_copy(
            stage.at[p], outs[i].at[pl.ds(n * length, length), :], out_sem.at[i])

    for step in ("start",) if g.full else ("start", "wait"):
        for i, t in enumerate(targets):
            for n in range(g.cap):
                p = order[t * g.cap + n]
                if g.full:
                    page_copy(i, n, p).start()
                else:
                    @pl.when(p >= 0)
                    def _():
                        getattr(page_copy(i, n, p), step)()
    base, passes = g.cap * length, []
    for c, size in enumerate(passed):
        arrivals[c].wait()
        for i in range(number):
            passes.append(pltpu.make_async_copy(
                pass_stages[c].at[i], outs[i].at[pl.ds(base, g.cap * size), :], pass_out.at[c, i]))
            passes[-1].start()
        base += g.cap * size
    if g.full:
        for i in range(len(targets)):
            block = outs[i].at[pl.ds(0, g.cap * length), :]
            pltpu.make_async_copy(block, block, out_sem.at[i]).wait()
    for copy in passes:
        copy.wait()


def pack(g, ks, dests, old, pieces, received, tail=None, label=False, single=True,
         passed=(), forwarded=()):
    _, length = spread(pieces)
    extra = LABEL_ROWS if label else (tail.shape[1] if tail is not None else 0)
    blocks = [received[c][j] for j in range(g.groups - 1) for c in range(len(pieces))]
    operands = [*dests, old, *blocks, *forwarded] + ([tail] if tail is not None else [])
    shape = (g.cap * (length + sum(passed)) + extra, 128)
    number = g.peers if ks is None else len(ks)
    if single:
        outs = [jax.ShapeDtypeStruct((number,) + shape, jnp.bfloat16)]
    else:
        outs = [jax.ShapeDtypeStruct(shape, jnp.bfloat16)] * number
    scratch = [
        pltpu.VMEM((g.page_count, length, 128), jnp.bfloat16),
        pltpu.SMEM((g.peers,), jnp.int32),
        pltpu.SMEM((g.peers * g.cap,), jnp.int32),
        pltpu.SMEM((g.peers * g.cap,), jnp.int32),
        pltpu.SemaphoreType.DMA((len(pieces) * g.groups,)),
        pltpu.SemaphoreType.DMA((number,)),
    ]
    scratch += [pltpu.VMEM((number, g.cap * size, 128), jnp.bfloat16) for size in passed]
    if passed:
        scratch += [pltpu.SemaphoreType.DMA((len(passed),)),
                    pltpu.SemaphoreType.DMA((len(passed), number))]
    return pl.pallas_call(
        functools.partial(pack_kernel, g, ks, single, pieces, passed, extra, label),
        out_shape=outs,
        in_specs=[SMEM] * g.groups + [HBM] * (1 + len(blocks) + len(forwarded))
        + ([VMEM] if tail is not None else []),
        out_specs=[HBM if passed else VMEM] * len(outs),
        scratch_shapes=scratch,
        cost_estimate=estimate(4 * number * g.cap * length * 128),
        name="pack",
    )(*operands)


def labels_kernel(g, row, blocks, out, raw, lines, sem, out_sem):
    copy = pltpu.make_async_copy(blocks.at[:, pl.ds(row, LABEL_ROWS), :], raw, sem)
    copy.start()
    copy.wait()
    for i in range(g.peers):
        lines[i:i + 1, :] = raw[i].astype(jnp.float32)[:1].astype(jnp.int32)
    move = pltpu.make_async_copy(lines, out, out_sem)
    move.start()
    move.wait()


def read_labels(g, blocks, row):
    return pl.pallas_call(
        functools.partial(labels_kernel, g, row),
        out_shape=jax.ShapeDtypeStruct((g.peers, 128), jnp.int32),
        in_specs=[HBM],
        out_specs=SMEM,
        scratch_shapes=[
            pltpu.VMEM((g.peers, LABEL_ROWS, 128), jnp.bfloat16),
            pltpu.VMEM((g.peers, 128), jnp.int32),
            pltpu.SemaphoreType.DMA,
            pltpu.SemaphoreType.DMA,
        ],
        compiler_params=granted(),
        cost_estimate=estimate(g.peers * 4096),
        name="labels",
    )(blocks)


def merge_partials(tails, attended, local, width, rows):
    lane = lax.broadcasted_iota(jnp.int32, (rows, 128), 1)
    diagonal = lane == lax.broadcasted_iota(jnp.int32, (rows, 128), 0)
    shared = 128 // width
    parts = (local + shared - 1) // shared * rows
    lines = [tail[parts:, :].astype(jnp.float32) for tail in tails]
    weights = []
    for s in range(local):
        logs = [jnp.sum(line[3 * s:3 * s + 3], axis=0, keepdims=True) for line in lines]
        top = functools.reduce(jnp.maximum, logs)
        scales = [jnp.exp(log - top) for log in logs]
        total = sum(scales)
        weights.append([scale / total for scale in scales])
    group = attended.shape[2] // width
    for first in range(0, local, shared):
        summed = jnp.zeros((rows, 128), jnp.float32)
        held = range(first, min(first + shared, local))
        for t, tail in enumerate(tails):
            scale = jnp.zeros((rows, 128), jnp.float32)
            for s in held:
                line = jnp.where(diagonal, jnp.broadcast_to(weights[s][t], (rows, 128)), 0.0)
                column = jnp.broadcast_to(jnp.sum(line, axis=1, keepdims=True), (rows, 128))
                scale = jnp.where(lane < 128 - width * (s - first), column, scale)
            row = first // shared * rows
            summed = summed + scale * tail[row:row + rows, :].astype(jnp.float32)
        for s in held:
            end = 128 - width * (s - first)
            values = summed[:, end - width:end].astype(jnp.bfloat16)
            for row in range(rows):
                k, j = row // group, row % group
                attended[s, k:k + 1, j * width:(j + 1) * width] = values[row:row + 1]


def place_kernel(g, ks, pieces, passed, first, merged, tail_rows, *refs):
    laid, length = spread(pieces)
    labels, refs = refs[0], refs[1:]
    me = lax.axis_index("seq")
    if ks is None:
        blocks, refs = [refs[0].at[t] for t in range(g.peers)], refs[1:]
        indices = list(range(g.peers))
    else:
        blocks, refs = refs[:len(ks)], refs[len(ks):]
        indices = [sender(me, k, g.peers) for k in ks]
    refs = refs if first else refs[1:]
    cache, refs = refs[0], refs[1:]
    if merged:
        attended, refs = refs[0], refs[1:]
    out_sem = refs[0]

    def each_page(act):
        for i, (block, index) in enumerate(zip(blocks, indices)):
            for n in range(g.cap):
                label = labels[index, n]

                def run():
                    for start, size, offset in laid:
                        getattr(pltpu.make_async_copy(
                            block.at[pl.ds(n * length + offset, size), :],
                            cache.at[label, pl.ds(start, size), :], out_sem.at[i]), act)()

                if g.full:
                    run()
                else:
                    pl.when(label >= 0)(run)
                if not passed:
                    continue
                other = labels[sender(index, g.peers // 2, g.peers), n]

                def run_passed():
                    base = g.cap * length
                    for start, size in passed:
                        getattr(pltpu.make_async_copy(
                            block.at[pl.ds(base + n * size, size), :],
                            cache.at[other, pl.ds(start, size), :], out_sem.at[i]), act)()
                        base += g.cap * size

                if g.full:
                    run_passed()
                else:
                    pl.when(other >= 0)(run_passed)

    each_page("start")
    if merged:
        merge_partials([block.at[pl.ds(g.cap * length, tail_rows), :] for block in blocks],
                       attended, *merged)
    if g.full:
        for i, block in enumerate(blocks):
            rows = g.cap * (length + sum(size for _, size in passed))
            moved = block.at[pl.ds(0, rows), :]
            pltpu.make_async_copy(moved, moved, out_sem.at[i]).wait()
    else:
        each_page("wait")


def place(g, ks, labels, blocks, cache, pieces, passed=(), merged=None, shape=None):
    first = cache is None
    _, length = spread(pieces)
    operands = [labels, *blocks] + ([] if first else [cache])
    outs = [jax.ShapeDtypeStruct((g.page_count, g.rows, 128), jnp.bfloat16)]
    out_specs = [HBM]
    if merged:
        outs.append(jax.ShapeDtypeStruct(shape, jnp.bfloat16))
        out_specs.append(VMEM)
    number = g.peers if ks is None else len(ks)
    return pl.pallas_call(
        functools.partial(place_kernel, g, ks, pieces, passed, first, merged,
                          blocks[0].shape[-2] - g.cap * length),
        out_shape=outs,
        in_specs=[SMEM] + [VMEM] * len(blocks) + [HBM] * (0 if first else 1),
        out_specs=out_specs,
        scratch_shapes=[pltpu.SemaphoreType.DMA((number,))],
        compiler_params=granted(2 * number * blocks[0].shape[-2] * 128),
        input_output_aliases={} if first else {len(operands) - 1: 0},
        cost_estimate=estimate(4 * number * g.cap * length * 128),
        name="place",
    )(*operands)


def attend_kernel(g, chunks, page_len, width, local, *refs):
    owner, fill, query, old = refs[:4]
    blocks = refs[4:4 + len(chunks) * (g.groups - 1)]
    (out, stage, scores, seq_lane, seq_max, seq_total, seq_sum, sems) = refs[4 + len(blocks):]
    seqs, kj, _ = query.shape
    heads = g.rows // page_len
    group = kj // heads
    offset = pl.multiple_of(lax.axis_index("head") * g.rows, 8)
    copies = [pltpu.make_async_copy(
        old.at[:, pl.ds(offset, g.rows), :], stage.at[pl.ds(0, g.pages_own)], sems.at[0])]
    for j in range(1, g.groups):
        for c, (start, length) in enumerate(chunks):
            i = (j - 1) * len(chunks) + c
            copies.append(pltpu.make_async_copy(
                blocks[i], stage.at[pl.ds(j * g.pages_own, g.pages_own), pl.ds(start, length), :],
                sems.at[i + 1]))
    for copy in copies:
        copy.start()
    seq_lane[...] = jnp.full_like(seq_lane, NEG_FILL)
    seq_total[...] = jnp.zeros_like(seq_total)
    seq_sum[...] = jnp.zeros_like(seq_sum)
    for copy in copies:
        copy.wait()
    token = lax.broadcasted_iota(jnp.int32, (kj, page_len), 1)
    scale = width ** -0.5

    def page(p, k):
        return stage[p, k * page_len:(k + 1) * page_len, :]

    @pl.loop(0, g.page_count, unroll=8)
    def _(p):
        s = owner[p]
        query_rows = query[s]
        tiles = [lax.dot_general(
            query_rows[k * group:(k + 1) * group], page(p, k), (((1,), (1,)), ((), ())),
            preferred_element_type=jnp.float32) for k in range(heads)]
        tile = jnp.concatenate(tiles, 0) * scale
        tile = jnp.where(token < fill[p], tile, NEG_FILL)
        scores[p] = tile
        seq_lane[s] = jnp.maximum(seq_lane[s], tile)

    @pl.loop(0, seqs, unroll=4)
    def _(s):
        seq_max[s] = jnp.broadcast_to(
            jnp.max(seq_lane[s], axis=1, keepdims=True), (kj, page_len))

    @pl.loop(0, g.page_count, unroll=8)
    def _(p):
        s = owner[p]
        tile = scores[p]
        live = token < fill[p]
        weights = jnp.where(live, jnp.exp(tile - seq_max[s]), 0.0)
        high = weights.astype(jnp.bfloat16)
        low = (weights - high.astype(jnp.float32)).astype(jnp.bfloat16)
        sums = []
        for k in range(heads):
            here = slice(k * group, (k + 1) * group)
            both = jnp.dot(jnp.concatenate([high[here], low[here]], 0), page(p, k),
                           preferred_element_type=jnp.float32)
            sums.append(both[:group] + both[group:])
        seq_total[s] = seq_total[s] + weights
        seq_sum[s] = seq_sum[s] + jnp.concatenate(sums, 0)

    lane = lax.broadcasted_iota(jnp.int32, (kj, 128), 1)
    diagonal = lane == lax.broadcasted_iota(jnp.int32, (kj, 128), 0)
    shared = 128 // width

    @pl.loop(0, g.peers)
    def _(t):
        lines = []
        for i in range(local):
            s = t * local + i
            total = jnp.sum(seq_total[s], axis=1, keepdims=True)
            some = total > 0.0
            safe = jnp.where(some, total, 1.0)
            value = jnp.where(some, seq_sum[s] / safe, 0.0)
            if i % shared:
                value = pltpu.roll(value, 128 - width * (i % shared), 1)
                value = jnp.where(lane < 128 - width * (i % shared), value, tile)
            tile = value
            if i % shared == shared - 1 or i == local - 1:
                row = i // shared * kj
                out[t, row:row + kj, :] = tile.astype(jnp.bfloat16)
            log = jnp.where(some, seq_max[s, :, :1] + jnp.log(safe), NEG_FILL)
            log = jnp.broadcast_to(log, (kj, 128))
            for _ in range(3):
                part = log.astype(jnp.bfloat16).astype(jnp.float32)
                log = log - part
                lines.append(jnp.sum(jnp.where(diagonal, part, 0.0), axis=0, keepdims=True))
        while len(lines) % 8:
            lines.append(jnp.zeros((1, 128), jnp.float32))
        parts = (local + shared - 1) // shared * kj
        out[t, parts:parts + len(lines), :] = jnp.concatenate(lines, 0).astype(jnp.bfloat16)


def attend(g, owner, fill, query, old, received, chunks, width, page_len):
    seqs, kj, _ = query.shape
    local = seqs // g.peers
    extra = -(-local // (128 // width)) * kj + (3 * local + 7) // 8 * 8
    blocks = [received[c][j] for j in range(g.groups - 1) for c in range(len(chunks))]
    return pl.pallas_call(
        functools.partial(attend_kernel, g, chunks, page_len, width, local),
        out_shape=jax.ShapeDtypeStruct((g.peers, extra, 128), jnp.bfloat16),
        in_specs=[SMEM, SMEM, VMEM] + [HBM] * (1 + len(blocks)),
        out_specs=VMEM,
        scratch_shapes=[
            pltpu.VMEM((g.page_count, g.rows, 128), jnp.bfloat16),
            pltpu.VMEM((g.page_count, kj, page_len), jnp.float32),
            pltpu.VMEM((seqs, kj, page_len), jnp.float32),
            pltpu.VMEM((seqs, kj, page_len), jnp.float32),
            pltpu.VMEM((seqs, kj, page_len), jnp.float32),
            pltpu.VMEM((seqs, kj, 128), jnp.float32),
            pltpu.SemaphoreType.DMA((len(blocks) + 1,)),
        ],
        cost_estimate=pl.CostEstimate(
            flops=g.page_count * kj * page_len * 512 * 16,
            bytes_accessed=2 * g.page_count * g.rows * 128,
            transcendentals=g.page_count * kj * page_len),
        name="attend",
    )(owner, fill, query, old, *blocks)


def page_layout(dest, seq_pages, last_fill, page_len, page_count, peers):
    position = dest % page_count * peers + dest // page_count
    seqs = seq_pages.shape[0]
    ids = jnp.arange(seqs, dtype=jnp.int32)
    ends = jnp.sum(jnp.where(ids[:, None] <= ids[None, :], seq_pages[:, None], 0), axis=0)
    owner = jnp.sum((position[:, None] >= ends[None, :]).astype(jnp.int32), axis=1)
    member = owner[:, None] == ids[None, :]
    last = jnp.any(member & (position[:, None] == ends[None, :] - 1), axis=1)
    owner_fill = jnp.sum(jnp.where(member, last_fill[None, :], 0), axis=1)
    return owner, jnp.where(last, owner_fill, page_len)


def per_device(old_cache, page_dest, seq_pages, last_fill, queries):
    pages_own, all_heads, page_len, double = old_cache.shape
    groups, peers = lax.axis_size("head"), lax.axis_size("seq")
    head = lax.axis_index("head").astype(jnp.int32)
    width = double // 2
    heads = all_heads // groups
    rows = heads * page_len
    g = Geometry(pages_own, groups, peers, rows)
    seqs = queries.shape[0]
    kj = heads * (queries.shape[2] // width)
    edges = [0]
    for c in range(1, len(SHARES) + 1):
        edges.append(max(rows * sum(SHARES[:c]) // sum(SHARES) // 8 * 8, edges[-1] + 8))
    chunks = tuple((a, b - a) for a, b in zip(edges, edges[1:]))
    last = len(chunks) - 1
    old = old_cache.reshape(pages_own, all_heads * page_len, double)

    def swap(x, j):
        return lax.ppermute(x, "head", [(i, (i + j) % groups) for i in range(groups)])

    far, near = tuple(range(peers // 2, peers)), tuple(range(peers // 2))

    def route(blocks, ks):
        return [block if k == 0 else lax.ppermute(
            block, "seq", [(i, partner(i, k, peers)) for i in range(peers)])
            for k, block in zip(ks, blocks)]

    dests = [page_dest] + [swap(page_dest, j) for j in range(1, groups)]
    dest = jnp.concatenate(dests)
    received, source = [], old
    for start, length in chunks:
        pieces = []
        for j in range(1, groups):
            other = (head + j) % groups
            pieces.append(lax.dynamic_slice(
                source, (0, other * rows + start, 0), (pages_own, length, double)))
        source, pieces = lax.optimization_barrier((source, pieces))
        received.append([swap(piece, j) for j, piece in enumerate(pieces, 1)])
    query = jnp.pad(queries.reshape(seqs, kj, width), ((0, 0), (0, 0), (0, double - width)))
    owner, fill = page_layout(dest, seq_pages, last_fill, page_len, g.page_count, peers)
    pack_args = (dests, old)
    incoming, forwarded, tail = [], {}, None
    first_all = KINDS.index("all")
    pending = []
    for c, (kind, chunk) in enumerate(zip(KINDS, chunks)):
        if c == last:
            tail = attend(g, owner, fill, query, old, received, chunks, width, page_len)
        blocks = pack(g, None if kind == "all" else far, *pack_args, (chunk,),
                      received[c:c + 1], tail, c == first_all, kind != "far")
        if kind == "all":
            blocks = [lax.all_to_all(
                blocks[0], "seq", split_axis=0, concat_axis=0, tiled=True)]
            incoming.append((None, blocks, (chunk,), ()))
        elif kind == "far":
            incoming.append((far, route(blocks, far), (chunk,), ()))
        else:
            forwarded[c] = route(blocks, far[:1])[0]
        if kind != "all":
            pending.append(c)
        if pending and kind != "fwd":
            passed = tuple(i for i in pending if i in forwarded)
            blocks = pack(g, near, *pack_args, tuple(chunks[i] for i in pending),
                          [received[i] for i in pending], single=False,
                          passed=tuple(chunks[i][1] for i in passed),
                          forwarded=[forwarded[i] for i in passed])
            blocks = route(blocks, near)
            incoming.append((near, blocks, tuple(chunks[i] for i in pending),
                             tuple(chunks[i] for i in passed)))
            pending = []
    labels = read_labels(g, incoming[0][1][0], g.cap * chunks[first_all][1])
    cache = None
    for i, (ks, blocks, pieces, passed) in enumerate(incoming):
        merged = (seqs // peers, width, kj) if i == len(incoming) - 1 else None
        shape = (seqs // peers, heads, kj // heads * width)
        cache, *attended = place(
            g, ks, labels, blocks, cache, pieces, passed, merged, shape)
    return cache.reshape(g.page_count, heads, page_len, double), attended[0]


def solution(mesh):
    in_specs = (
        P(("seq", "head"), None, None, None),
        P(("seq", "head")),
        P(),
        P(),
        P(None, "head", None),
    )
    out_specs = (P("seq", "head", None, None), P("seq", "head", None))
    return jax.shard_map(
        per_device, mesh=mesh, in_specs=in_specs, out_specs=out_specs, check_vma=False
    )
```

profile of v0, /device:TPU:0, one launch (start us, length us, event | category | flops | bytes accessed | tf_op | source)
XLA Modules:
  0.0 338.0 jit_solution(9290950751147806879)
XLA Ops:
  9.0 3.1 collective-permute-start.1
  12.1 23.2 %collective-permute-done.refs_1_ = s32[32]{0:T(128)S(1)} collective-permute-done((s32[32]{0:T(128)}, s32[32]{0:T(128)S(1)}, u32[]{:S(2)}, u32[]{:S(2)}) %collective-permute-start) | collective-permute-done | bytes 160 | tf_op jit(solution)/shard_map/ppermute | solution.py:506
  36.8 3.8 %pack.9 = bf16[16,520,128]{2,1,0:T(8,128)(2,1)} custom-call(s32[32]{0:T(128)} %refs_0_.17, s32[32]{0:T(128)} %copy-done.9, bf16[32,1024,128]{2,1,0:T(8,128)(2,1)} %bitcast.7, bf16[32,128,128]{2,1,0:T(8,128)(2,1)} %copy-done.3), custom_call_target="tpu_custom_call" | custom-call | flops 16777216 | bytes 4194304 | tf_op jit(solution)/shard_map/pack/pallas_call | solution.py:195
  40.6 6.1 %all-to-all-start = ((bf16[16,520,128]{2,1,0:T(8,128)(2,1)}), bf16[16,520,128]{2,1,0:T(8,128)(2,1)S(1)}, u32[]{:S(2)}, u32[]{:S(2)}) async-start(bf16[16,520,128]{2,1,0:T(8,128)(2,1)} %pack.9), calls=%async_computation | async-start | bytes 4259840 | tf_op jit(solution)/shard_map/all_to_all | solution.py:538
  59.1 14.1 %collective-permute-done.3.refs_4_.refs_3_ = bf16[32,16,128]{2,1,0:T(8,128)(2,1)} collective-permute-done((bf16[32,16,128]{2,1,0:T(8,128)(2,1)}, bf16[32,16,128]{2,1,0:T(8,128)(2,1)}, u32[]{:S(2)}, u32[]{:S(2)}) %collective-permute-start.3) | collective-permute-done | bytes 131104 | tf_op jit(solution)/shard_map/ppermute | solution.py:506
  75.4 42.0 %collective-permute-done.4.refs_5_.refs_3_.refs_4_ = bf16[32,32,128]{2,1,0:T(8,128)(2,1)S(1)} collective-permute-done((bf16[32,32,128]{2,1,0:T(8,128)(2,1)}, bf16[32,32,128]{2,1,0:T(8,128)(2,1)S(1)}, u32[]{:S(2)}, u32[]{:S(2)}) %collective-permute-start.4) | collective-permute-done | bytes 262176 | tf_op jit(solution)/shard_map/ppermute | solution.py:506
  119.1 17.6 %attend.1.refs_4_ = bf16[16,40,128]{2,1,0:T(8,128)(2,1)} custom-call(s32[64]{0:T(128)} %copy-done.11, s32[64]{0:T(128)} %broadcast_select_fusion.refs_1_, bf16[32,32,128]{2,1,0:T(8,128)(2,1)} %pad.4.refs_2_, bf16[32,1024,128]{2,1,0:T(8,128)(2,1)} %bitcast.10, bf16[32,16,128]{2,1,0:T(8,128)(2,1)} %collective-permute-done.3.refs_4_.refs_3_, ...), custom_call_target="tpu_custom_call" | custom-call | flops 2147483648 | bytes 8388608 | tf_op jit(solution)/shard_map/attend/pallas_call | solution.py:454
  136.7 3.8 %pack.10 = bf16[16,424,128]{2,1,0:T(8,128)(2,1)} custom-call(s32[32]{0:T(128)} %refs_0_.17, s32[32]{0:T(128)} %copy-done.9, bf16[32,1024,128]{2,1,0:T(8,128)(2,1)} %bitcast.11, bf16[32,96,128]{2,1,0:T(8,128)(2,1)} %collective-permute-done.2.refs_10_.refs_3_, bf16[16,40,128]{2,1,0:T(8,128)(2,1)} %attend.1.refs_4_), custom_call_target="tpu_custom_call" | custom-call | flops 12582912 | bytes 3145728 | tf_op jit(solution)/shard_map/pack/pallas_call | solution.py:195
  140.5 5.8 %all-to-all-start.1 = ((bf16[16,424,128]{2,1,0:T(8,128)(2,1)}), bf16[16,424,128]{2,1,0:T(8,128)(2,1)}, u32[]{:S(2)}, u32[]{:S(2)}) async-start(bf16[16,424,128]{2,1,0:T(8,128)(2,1)} %pack.10), calls=%async_computation.1 | async-start | bytes 3473408 | tf_op jit(solution)/shard_map/all_to_all | solution.py:538
  149.1 2.8 collective-permute-start.26
  157.4 2.8 collective-permute-start.24
  162.9 3.4 %pack.12 = (bf16[512,128]{1,0:T(8,128)(2,1)}, bf16[512,128]{1,0:T(8,128)(2,1)}, bf16[512,128]{1,0:T(8,128)(2,1)}, bf16[512,128]{1,0:T(8,128)(2,1)}, bf16[512,128...) custom-call(s32[32]{0:T(128)} %refs_0_.17, s32[32]{0:T(128)} %copy-done.9, ...), custom_call_target="tpu_custom_call" | custom-call | flops 8388608 | bytes 2097152 | tf_op jit(solution)/shard_map/pack/pallas_call | solution.py:195
  166.2 2.8 collective-permute-start.15
  169.1 78.0 %collective-permute-done.23.refs_7_ = bf16[8,64,128]{2,1,0:T(8,128)(2,1)S(1)} collective-permute-done((bf16[8,64,128]{2,1,0:T(8,128)(2,1)}, bf16[8,64,128]{2,1,0:T(8,128)(2,1)S(1)}, u32[]{:S(2)}, u32[]{:S(2)}) %collective-permute-start.23) | collective-permute-done | bytes 131104 | tf_op jit(solution)/shard_map/ppermute | solution.py:511
  252.3 4.7 %pack.17 = (bf16[1280,128]{1,0:T(8,128)(2,1)}, bf16[1280,128]{1,0:T(8,128)(2,1)}, bf16[1280,128]{1,0:T(8,128)(2,1)}, bf16[1280,128]{1,0:T(8,128)(2,1)}, bf16[128...) custom-call(s32[32]{0:T(128)} %refs_0_.17, ...), custom_call_target="tpu_custom_call" | custom-call | flops 10485760 | bytes 2621440 | tf_op jit(solution)/shard_map/pack/pallas_call | solution.py:195
  267.0 6.4 %collective-permute-done.18.refs_4_ = bf16[512,128]{1,0:T(8,128)(2,1)S(1)} collective-permute-done((bf16[512,128]{1,0:T(8,128)(2,1)}, bf16[512,128]{1,0:T(8,128)(2,1)S(1)}, u32[]{:S(2)}, u32[]{:S(2)}) %collective-permute-start.18) | collective-permute-done | bytes 131104 | tf_op jit(solution)/shard_map/ppermute | solution.py:511
  273.5 3.4 pack.11
  276.9 4.1 %collective-permute-start.22 = (bf16[512,128]{1,0:T(8,128)(2,1)}, bf16[512,128]{1,0:T(8,128)(2,1)S(1)}, u32[]{:S(2)}, u32[]{:S(2)}) collective-permute-start(bf16[512,128]{1,0:T(8,128)(2,1)} %get-tuple-element.69), channel_id=1, source_target_pairs={{0,30},{2,28},{4,26},{6,24},{8,22},{10,20},{12,18},{14,16},{16,14}... | collective-permute-start | bytes 393224 | tf_op jit(solution)/shard_map/ppermute | solution.py:511
  281.9 6.2 %collective-permute-start.11 = (bf16[512,128]{1,0:T(8,128)(2,1)}, bf16[512,128]{1,0:T(8,128)(2,1)S(1)}, u32[]{:S(2)}, u32[]{:S(2)}) collective-permute-start(bf16[512,128]{1,0:T(8,128)(2,1)} %get-tuple-element.58), channel_id=1, source_target_pairs={{0,8},{2,10},{4,12},{6,14},{8,0},{10,2},{12,4},{14,6},{16,24},{18,... | collective-permute-start | bytes 393224 | tf_op jit(solution)/shard_map/ppermute | solution.py:511
  288.8 3.2 collective-permute-start.30
  302.7 4.8 %collective-permute-done.31.refs_6_ = bf16[1280,128]{1,0:T(8,128)(2,1)S(1)} collective-permute-done((bf16[1280,128]{1,0:T(8,128)(2,1)}, bf16[1280,128]{1,0:T(8,128)(2,1)S(1)}, u32[]{:S(2)}, u32[]{:S(2)}) %collective-permute-start.31) | collective-permute-done | bytes 327712 | tf_op jit(solution)/shard_map/ppermute | solution.py:511
  309.2 5.6 %collective-permute-done.32.refs_7_ = bf16[1280,128]{1,0:T(8,128)(2,1)S(1)} collective-permute-done((bf16[1280,128]{1,0:T(8,128)(2,1)}, bf16[1280,128]{1,0:T(8,128)(2,1)S(1)}, u32[]{:S(2)}, u32[]{:S(2)}) %collective-permute-start.32) | collective-permute-done | bytes 327712 | tf_op jit(solution)/shard_map/ppermute | solution.py:511
  314.8 6.8 %collective-permute-done.33.refs_8_ = bf16[1280,128]{1,0:T(8,128)(2,1)S(1)} collective-permute-done((bf16[1280,128]{1,0:T(8,128)(2,1)}, bf16[1280,128]{1,0:T(8,128)(2,1)S(1)}, u32[]{:S(2)}, u32[]{:S(2)}) %collective-permute-start.33) | collective-permute-done | bytes 327712 | tf_op jit(solution)/shard_map/ppermute | solution.py:511
  334.5 3.5 %place.9 = (bf16[64,512,128]{2,1,0:T(8,128)(2,1)}, bf16[2,4,512]{2,1,0:T(4,128)(2,1)}) custom-call(s32[16,128]{1,0:T(8,128)S(1)} %labels.1.refs_0_, bf16[16,424,128]{2,1,0:T(8,128)(2,1)} %all-to-all-done.1.refs_1_, bf16[64,512,128]{2,1,0:T(8,128)(2,1)} %place.8.refs_2_), custom_call_target="tpu_custom_call", output_to_operand_aliasing={{0}: (2, {})} | custom-call | flops 12582912 | bytes 3145728 | tf_op jit(solution)/shard_map/place/pallas_call | solution.py:340
  (108 shorter events, 78.9 us)
Async XLA Ops:
  9.0 26.3 %collective-permute-start.1 = (bf16[32,128,128]{2,1,0:T(8,128)(2,1)S(1)}, bf16[32,128,128]{2,1,0:T(8,128)(2,1)S(1)}, u32[]{:S(2)}, u32[]{:S(2)}) collective-permute-start(bf16[32,128,128]{2,1,0:T(8,128)(2,1)S(1)} %constant_dynamic-slice_fusion.2), channel_id=1, source_target_pairs={{0,1},{1,0},{2,3},{3,2},{4,5},{5,4},{6,7},{7,6},{8,9},{9,8},{10,11... | collective-permute-start | bytes 3145736 | tf_op jit(solution)/shard_map/ppermute | solution.py:506
  12.0 23.3 %collective-permute-start = (s32[32]{0:T(128)}, s32[32]{0:T(128)S(1)}, u32[]{:S(2)}, u32[]{:S(2)}) collective-permute-start(s32[32]{0:T(128)} %refs_0_.17), channel_id=1, source_target_pairs={{0,1},{1,0},{2,3},{3,2},{4,5},{5,4},{6,7},{7,6},{8,9},{9,8},{10,11... | collective-permute-start | bytes 392 | tf_op jit(solution)/shard_map/ppermute | solution.py:506
  40.6 99.9 %all-to-all-start = ((bf16[16,520,128]{2,1,0:T(8,128)(2,1)}), bf16[16,520,128]{2,1,0:T(8,128)(2,1)S(1)}, u32[]{:S(2)}, u32[]{:S(2)}) async-start(bf16[16,520,128]{2,1,0:T(8,128)(2,1)} %pack.9), calls=%async_computation | async-start | bytes 4259840 | tf_op jit(solution)/shard_map/all_to_all | solution.py:538
  46.8 70.6 %collective-permute-start.6 = (bf16[32,64,128]{2,1,0:T(8,128)(2,1)}, bf16[32,64,128]{2,1,0:T(8,128)(2,1)}, u32[]{:S(2)}, u32[]{:S(2)}) collective-permute-start(bf16[32,64,128]{2,1,0:T(8,128)(2,1)} %constant_dynamic-slice_fusion.3), channel_id=1, source_target_pairs={{0,1},{1,0},{2,3},{3,2},{4,5},{5,4},{6,7},{7,6},{8,9},{9,8},{10,11... | collective-permute-start | bytes 1572872 | tf_op jit(solution)/shard_map/ppermute | solution.py:506
  48.4 69.0 %collective-permute-start.5 = (bf16[32,48,128]{2,1,0:T(8,128)(2,1)}, bf16[32,48,128]{2,1,0:T(8,128)(2,1)}, u32[]{:S(2)}, u32[]{:S(2)}) collective-permute-start(bf16[32,48,128]{2,1,0:T(8,128)(2,1)} %constant_dynamic-slice_fusion.4), channel_id=1, source_target_pairs={{0,1},{1,0},{2,3},{3,2},{4,5},{5,4},{6,7},{7,6},{8,9},{9,8},{10,11... | collective-permute-start | bytes 1179656 | tf_op jit(solution)/shard_map/ppermute | solution.py:506
  48.9 24.3 %collective-permute-start.3 = (bf16[32,16,128]{2,1,0:T(8,128)(2,1)}, bf16[32,16,128]{2,1,0:T(8,128)(2,1)}, u32[]{:S(2)}, u32[]{:S(2)}) collective-permute-start(bf16[32,16,128]{2,1,0:T(8,128)(2,1)} %constant_dynamic-slice_fusion.6), channel_id=1, source_target_pairs={{0,1},{1,0},{2,3},{3,2},{4,5},{5,4},{6,7},{7,6},{8,9},{9,8},{10,11... | collective-permute-start | bytes 393224 | tf_op jit(solution)/shard_map/ppermute | solution.py:506
  52.7 64.7 %collective-permute-start.7 = (bf16[32,128,128]{2,1,0:T(8,128)(2,1)}, bf16[32,128,128]{2,1,0:T(8,128)(2,1)S(1)}, u32[]{:S(2)}, u32[]{:S(2)}) collective-permute-start(bf16[32,128,128]{2,1,0:T(8,128)(2,1)} %constant_dynamic-slice_fusion.1), channel_id=1, source_target_pairs={{0,1},{1,0},{2,3},{3,2},{4,5},{5,4},{6,7},{7,6},{8,9},{9,8},{10,11... | collective-permute-start | bytes 3145736 | tf_op jit(solution)/shard_map/ppermute | solution.py:506
  55.3 62.1 %collective-permute-start.2 = (bf16[32,96,128]{2,1,0:T(8,128)(2,1)}, bf16[32,96,128]{2,1,0:T(8,128)(2,1)}, u32[]{:S(2)}, u32[]{:S(2)}) collective-permute-start(bf16[32,96,128]{2,1,0:T(8,128)(2,1)} %constant_dynamic-slice_fusion), channel_id=1, source_target_pairs={{0,1},{1,0},{2,3},{3,2},{4,5},{5,4},{6,7},{7,6},{8,9},{9,8},{10,11... | collective-permute-start | bytes 2359304 | tf_op jit(solution)/shard_map/ppermute | solution.py:506
  73.2 44.2 %collective-permute-start.4 = (bf16[32,32,128]{2,1,0:T(8,128)(2,1)}, bf16[32,32,128]{2,1,0:T(8,128)(2,1)S(1)}, u32[]{:S(2)}, u32[]{:S(2)}) collective-permute-start(bf16[32,32,128]{2,1,0:T(8,128)(2,1)} %constant_dynamic-slice_fusion.5), channel_id=1, source_target_pairs={{0,1},{1,0},{2,3},{3,2},{4,5},{5,4},{6,7},{7,6},{8,9},{9,8},{10,11... | collective-permute-start | bytes 786440 | tf_op jit(solution)/shard_map/ppermute | solution.py:506
  140.5 194.0 %all-to-all-start.1 = ((bf16[16,424,128]{2,1,0:T(8,128)(2,1)}), bf16[16,424,128]{2,1,0:T(8,128)(2,1)}, u32[]{:S(2)}, u32[]{:S(2)}) async-start(bf16[16,424,128]{2,1,0:T(8,128)(2,1)} %pack.10), calls=%async_computation.1 | async-start | bytes 3473408 | tf_op jit(solution)/shard_map/all_to_all | solution.py:538
  149.1 102.4 %collective-permute-start.26 = (bf16[8,256,128]{2,1,0:T(8,128)(2,1)}, bf16[8,256,128]{2,1,0:T(8,128)(2,1)S(1)}, u32[]{:S(2)}, u32[]{:S(2)}) collective-permute-start(bf16[8,256,128]{2,1,0:T(8,128)(2,1)} %pack.16), channel_id=1, source_target_pairs={{0,16},{2,18},{4,20},{6,22},{8,24},{10,26},{12,28},{14,30},{16,0},... | collective-permute-start | bytes 1572872 | tf_op jit(solution)/shard_map/ppermute | solution.py:511
  154.6 95.6 %collective-permute-start.25 = (bf16[8,192,128]{2,1,0:T(8,128)(2,1)}, bf16[8,192,128]{2,1,0:T(8,128)(2,1)}, u32[]{:S(2)}, u32[]{:S(2)}) collective-permute-start(bf16[8,192,128]{2,1,0:T(8,128)(2,1)} %pack.15), channel_id=1, source_target_pairs={{0,16},{2,18},{4,20},{6,22},{8,24},{10,26},{12,28},{14,30},{16,0},... | collective-permute-start | bytes 1179656 | tf_op jit(solution)/shard_map/ppermute | solution.py:511
  157.4 90.4 %collective-permute-start.24 = (bf16[8,128,128]{2,1,0:T(8,128)(2,1)}, bf16[8,128,128]{2,1,0:T(8,128)(2,1)S(1)}, u32[]{:S(2)}, u32[]{:S(2)}) collective-permute-start(bf16[8,128,128]{2,1,0:T(8,128)(2,1)} %pack.14), channel_id=1, source_target_pairs={{0,16},{2,18},{4,20},{6,22},{8,24},{10,26},{12,28},{14,30},{16,0},... | collective-permute-start | bytes 786440 | tf_op jit(solution)/shard_map/ppermute | solution.py:511
  162.6 84.5 %collective-permute-start.23 = (bf16[8,64,128]{2,1,0:T(8,128)(2,1)}, bf16[8,64,128]{2,1,0:T(8,128)(2,1)S(1)}, u32[]{:S(2)}, u32[]{:S(2)}) collective-permute-start(bf16[8,64,128]{2,1,0:T(8,128)(2,1)} %pack.13), channel_id=1, source_target_pairs={{0,16},{2,18},{4,20},{6,22},{8,24},{10,26},{12,28},{14,30},{16,0},... | collective-permute-start | bytes 393224 | tf_op jit(solution)/shard_map/ppermute | solution.py:511
  166.2 91.1 %collective-permute-start.15 = (bf16[512,128]{1,0:T(8,128)(2,1)}, bf16[512,128]{1,0:T(8,128)(2,1)S(1)}, u32[]{:S(2)}, u32[]{:S(2)}) collective-permute-start(bf16[512,128]{1,0:T(8,128)(2,1)} %get-tuple-element.62), channel_id=1, source_target_pairs={{0,16},{2,18},{4,20},{6,22},{8,24},{10,26},{12,28},{14,30},{16,0},... | collective-permute-start | bytes 393224 | tf_op jit(solution)/shard_map/ppermute | solution.py:511
  247.8 17.2 %collective-permute-start.17 = (bf16[512,128]{1,0:T(8,128)(2,1)}, bf16[512,128]{1,0:T(8,128)(2,1)S(1)}, u32[]{:S(2)}, u32[]{:S(2)}) collective-permute-start(bf16[512,128]{1,0:T(8,128)(2,1)} %get-tuple-element.64), channel_id=1, source_target_pairs={{0,20},{2,22},{4,16},{6,18},{8,28},{10,30},{12,24},{14,26},{16,4},... | collective-permute-start | bytes 393224 | tf_op jit(solution)/shard_map/ppermute | solution.py:511
  250.2 23.2 %collective-permute-start.18 = (bf16[512,128]{1,0:T(8,128)(2,1)}, bf16[512,128]{1,0:T(8,128)(2,1)S(1)}, u32[]{:S(2)}, u32[]{:S(2)}) collective-permute-start(bf16[512,128]{1,0:T(8,128)(2,1)} %get-tuple-element.65), channel_id=1, source_target_pairs={{0,22},{2,20},{4,18},{6,16},{8,30},{10,28},{12,26},{14,24},{16,6},... | collective-permute-start | bytes 393224 | tf_op jit(solution)/shard_map/ppermute | solution.py:511
  257.0 35.6 %collective-permute-start.27 = (bf16[1280,128]{1,0:T(8,128)(2,1)}, bf16[1280,128]{1,0:T(8,128)(2,1)S(1)}, u32[]{:S(2)}, u32[]{:S(2)}) collective-permute-start(bf16[1280,128]{1,0:T(8,128)(2,1)} %get-tuple-element.71), channel_id=1, source_target_pairs={{0,2},{2,0},{4,6},{6,4},{8,10},{10,8},{12,14},{14,12},{16,18},{18,... | collective-permute-start | bytes 983048 | tf_op jit(solution)/shard_map/ppermute | solution.py:511
  257.4 36.5 %collective-permute-start.28 = (bf16[1280,128]{1,0:T(8,128)(2,1)}, bf16[1280,128]{1,0:T(8,128)(2,1)S(1)}, u32[]{:S(2)}, u32[]{:S(2)}) collective-permute-start(bf16[1280,128]{1,0:T(8,128)(2,1)} %get-tuple-element.72), channel_id=1, source_target_pairs={{0,4},{2,6},{4,0},{6,2},{8,12},{10,14},{12,8},{14,10},{16,20},{18,... | collective-permute-start | bytes 983048 | tf_op jit(solution)/shard_map/ppermute | solution.py:511
  292.6 22.2 %collective-permute-start.32 = (bf16[1280,128]{1,0:T(8,128)(2,1)}, bf16[1280,128]{1,0:T(8,128)(2,1)S(1)}, u32[]{:S(2)}, u32[]{:S(2)}) collective-permute-start(bf16[1280,128]{1,0:T(8,128)(2,1)} %get-tuple-element.76), channel_id=1, source_target_pairs={{0,12},{2,14},{4,8},{6,10},{8,4},{10,6},{12,0},{14,2},{16,28},{18,... | collective-permute-start | bytes 983048 | tf_op jit(solution)/shard_map/ppermute | solution.py:511
  293.8 27.7 %collective-permute-start.33 = (bf16[1280,128]{1,0:T(8,128)(2,1)}, bf16[1280,128]{1,0:T(8,128)(2,1)S(1)}, u32[]{:S(2)}, u32[]{:S(2)}) collective-permute-start(bf16[1280,128]{1,0:T(8,128)(2,1)} %get-tuple-element.77), channel_id=1, source_target_pairs={{0,14},{2,12},{4,10},{6,8},{8,6},{10,4},{12,2},{14,0},{16,30},{18,... | collective-permute-start | bytes 983048 | tf_op jit(solution)/shard_map/ppermute | solution.py:511
  298.3 32.2 %collective-permute-start.12 = (bf16[512,128]{1,0:T(8,128)(2,1)}, bf16[512,128]{1,0:T(8,128)(2,1)S(1)}, u32[]{:S(2)}, u32[]{:S(2)}) collective-permute-start(bf16[512,128]{1,0:T(8,128)(2,1)} %get-tuple-element.59), channel_id=1, source_target_pairs={{0,10},{2,8},{4,14},{6,12},{8,2},{10,0},{12,6},{14,4},{16,26},{18,... | collective-permute-start | bytes 393224 | tf_op jit(solution)/shard_map/ppermute | solution.py:511
  300.8 29.7 %collective-permute-start.13 = (bf16[512,128]{1,0:T(8,128)(2,1)}, bf16[512,128]{1,0:T(8,128)(2,1)S(1)}, u32[]{:S(2)}, u32[]{:S(2)}) collective-permute-start(bf16[512,128]{1,0:T(8,128)(2,1)} %get-tuple-element.60), channel_id=1, source_target_pairs={{0,12},{2,14},{4,8},{6,10},{8,4},{10,6},{12,0},{14,2},{16,28},{18,... | collective-permute-start | bytes 393224 | tf_op jit(solution)/shard_map/ppermute | solution.py:511
  307.5 23.0 %collective-permute-start.14 = (bf16[512,128]{1,0:T(8,128)(2,1)}, bf16[512,128]{1,0:T(8,128)(2,1)S(1)}, u32[]{:S(2)}, u32[]{:S(2)}) collective-permute-start(bf16[512,128]{1,0:T(8,128)(2,1)} %get-tuple-element.61), channel_id=1, source_target_pairs={{0,14},{2,12},{4,10},{6,8},{8,6},{10,4},{12,2},{14,0},{16,30},{18,... | collective-permute-start | bytes 393224 | tf_op jit(solution)/shard_map/ppermute | solution.py:511
  (26 other events, 449.5 us)
where the time goes:
time: 339 us; the launch traced here: 338 us
  waiting for transfers between devices  190 us (56%)
  starting transfers between devices  66.5 us (20%)
  Pallas kernels  60.3 us (18%)
  local copies, waits for them, and re-layouts  19.2 us (6%)
    ppermute x26, waiting for transfers between devices, route(): lax.ppermute(block, 'seq', [(i, partner(i, k, peers)) for i in range(peer...  111 us
    ppermute x8, waiting for transfers between devices, swap(): lax.ppermute(x, 'head', [(i, (i + j) % groups) for i in range(groups)])  79.3 us
    ppermute x26, starting transfers between devices, route(): lax.ppermute(block, 'seq', [(i, partner(i, k, peers)) for i in range(peer...  44.3 us
    pallas_call x9, Pallas kernels, pack(): pl.pallas_call(functools.partial(pack_kernel, g, ks, single, pieces, pass...  29.5 us
    pallas_call x1, Pallas kernels, attend(): pl.pallas_call(functools.partial(attend_kernel, g, chunks, page_len, widt...  17.6 us
    dynamic_slice x7, local copies, waits for them, and re-layouts, per_device(): lax.dynamic_slice(source, (0, other * rows + start, 0), (pages_own, lengt...  12.7 us
    all_to_all x2, starting transfers between devices, per_device(): lax.all_to_all(blocks[0], 'seq', split_axis=0, concat_axis=0, tiled=True)  11.9 us
    pallas_call x5, Pallas kernels, place(): pl.pallas_call(functools.partial(place_kernel, g, ks, pieces, passed, fir...  11.7 us
  transfers between devices with their start and end apart: 36, of which 13 were waited for; matrix products, arithmetic and copies ran while one was open for 2% of the time, Pallas kernels for 16%

commit v1 on v0

--- a/solution.py
+++ b/solution.py
@@ -8,7 +8,7 @@
 
 NEG_FILL = -1e30
 LABEL_ROWS = 8
-SHARES = (1, 2, 3, 4, 8, 8, 6)
+SHARES = (1, 2, 3, 4, 8, 9, 5)
 KINDS = ("fwd", "fwd", "fwd", "fwd", "all", "far", "all")
 
 HBM = pl.BlockSpec(memory_space=pltpu.HBM)
@@ -119,7 +119,8 @@
     for i, t in enumerate(targets):
         block = outs[i]
         if tail is not None:
-            block[g.cap * length:, :] = tail[t]
+            block[g.cap * length:g.cap * length + extra // 2, :] = tail[t]
+            block[g.cap * length + extra // 2:, :] = tail[partner(t, g.peers // 2, g.peers)]
         if label:
             lane = lax.broadcasted_iota(jnp.int32, (extra, 128), 1)
             tile = jnp.full((extra, 128), -1, jnp.int32)
@@ -171,7 +172,7 @@
 def pack(g, ks, dests, old, pieces, received, tail=None, label=False, single=True,
          passed=(), forwarded=()):
     _, length = spread(pieces)
-    extra = LABEL_ROWS if label else (tail.shape[1] if tail is not None else 0)
+    extra = LABEL_ROWS if label else (2 * tail.shape[1] if tail is not None else 0)
     blocks = [received[c][j] for j in range(g.groups - 1) for c in range(len(pieces))]
     operands = [*dests, old, *blocks, *forwarded] + ([tail] if tail is not None else [])
     shape = (g.cap * (length + sum(passed)) + extra, 128)
@@ -233,40 +234,83 @@
     )(blocks)
 
 
-def merge_partials(tails, attended, local, width, rows):
-    lane = lax.broadcasted_iota(jnp.int32, (rows, 128), 1)
-    diagonal = lane == lax.broadcasted_iota(jnp.int32, (rows, 128), 0)
-    shared = 128 // width
-    parts = (local + shared - 1) // shared * rows
-    lines = [tail[parts:, :].astype(jnp.float32) for tail in tails]
-    weights = []
+def entry_rows(local, kj):
+    return local * kj + (3 * local + 7) // 8 * 8
+
+
+def write_entries(out, entries, width):
+    kj = entries[0][0].shape[0]
+    lane = lax.broadcasted_iota(jnp.int32, (kj, 128), 1)
+    diagonal = lane == lax.broadcasted_iota(jnp.int32, (kj, 128), 0)
+    lines = []
+    for i, (value, log) in enumerate(entries):
+        high = value.astype(jnp.bfloat16).astype(jnp.float32)
+        low = pltpu.roll(value - high, 128 - width, 1)
+        out[i * kj:(i + 1) * kj, :] = jnp.where(lane < width, low, high).astype(jnp.bfloat16)
+        for _ in range(3):
+            part = log.astype(jnp.bfloat16).astype(jnp.float32)
+            log = log - part
+            lines.append(jnp.sum(jnp.where(diagonal, part, 0.0), axis=0, keepdims=True))
+    while len(lines) % 8:
+        lines.append(jnp.zeros((1, 128), jnp.float32))
+    row = len(entries) * kj
+    out[row:row + len(lines), :] = jnp.concatenate(lines, 0).astype(jnp.bfloat16)
+
+
+def merge_entries(tails, local, width, kj):
+    lane = lax.broadcasted_iota(jnp.int32, (kj, 128), 1)
+    diagonal = lane == lax.broadcasted_iota(jnp.int32, (kj, 128), 0)
+
+    def column(line):
+        spread_line = jnp.where(diagonal, jnp.broadcast_to(line, (kj, 128)), 0.0)
+        return jnp.broadcast_to(jnp.sum(spread_line, axis=1, keepdims=True), (kj, 128))
+
+    lines = [tail[local * kj:, :].astype(jnp.float32) for tail in tails]
+    merged = []
     for s in range(local):
         logs = [jnp.sum(line[3 * s:3 * s + 3], axis=0, keepdims=True) for line in lines]
         top = functools.reduce(jnp.maximum, logs)
         scales = [jnp.exp(log - top) for log in logs]
         total = sum(scales)
-        weights.append([scale / total for scale in scales])
-    group = attended.shape[2] // width
-    for first in range(0, local, shared):
-        summed = jnp.zeros((rows, 128), jnp.float32)
-        held = range(first, min(first + shared, local))
-        for t, tail in enumerate(tails):
-            scale = jnp.zeros((rows, 128), jnp.float32)
-            for s in held:
-                line = jnp.where(diagonal, jnp.broadcast_to(weights[s][t], (rows, 128)), 0.0)
-                column = jnp.broadcast_to(jnp.sum(line, axis=1, keepdims=True), (rows, 128))
-                scale = jnp.where(lane < 128 - width * (s - first), column, scale)
-            row = first // shared * rows
-            summed = summed + scale * tail[row:row + rows, :].astype(jnp.float32)
-        for s in held:
-            end = 128 - width * (s - first)
-            values = summed[:, end - width:end].astype(jnp.bfloat16)
-            for row in range(rows):
-                k, j = row // group, row % group
-                attended[s, k:k + 1, j * width:(j + 1) * width] = values[row:row + 1]
-
-
-def place_kernel(g, ks, pieces, passed, first, merged, tail_rows, *refs):
+        summed = jnp.zeros((kj, 128), jnp.float32)
+        for tail, scale in zip(tails, scales):
+            summed = summed + column(scale / total) * tail[s * kj:(s + 1) * kj, :].astype(jnp.float32)
+        merged.append((summed + pltpu.roll(summed, width, 1), column(top + jnp.log(total))))
+    return merged
+
+
+def reduce_kernel(row, local, width, kj, *refs):
+    blocks, (mine, across, tail, sems) = refs[:-4], refs[-4:]
+    extra = entry_rows(local, kj)
+    copies = [pltpu.make_async_copy(block.at[pl.ds(row, 2 * extra), :], tail.at[i], sems.at[i])
+              for i, block in enumerate(blocks)]
+    for copy in copies:
+        copy.start()
+    for copy in copies:
+        copy.wait()
+    for out, first in ((mine, 0), (across, extra)):
+        tails = [tail[i, first:first + extra, :] for i in range(len(blocks))]
+        write_entries(out, merge_entries(tails, local, width, kj), width)
+
+
+def reduce_near(blocks, row, local, width, kj):
+    extra = entry_rows(local, kj)
+    return pl.pallas_call(
+        functools.partial(reduce_kernel, row, local, width, kj),
+        out_shape=[jax.ShapeDtypeStruct((extra, 128), jnp.bfloat16)] * 2,
+        in_specs=[HBM] * len(blocks),
+        out_specs=[VMEM] * 2,
+        scratch_shapes=[
+            pltpu.VMEM((len(blocks), 2 * extra, 128), jnp.bfloat16),
+            pltpu.SemaphoreType.DMA((len(blocks),)),
+        ],
+        compiler_params=granted(2 * len(blocks) * 2 * extra * 128),
+        cost_estimate=estimate(len(blocks) * extra * 2048),
+        name="reduce",
+    )(*blocks)
+
+
+def place_kernel(g, ks, pieces, passed, first, merged, *refs):
     laid, length = spread(pieces)
     labels, refs = refs[0], refs[1:]
     me = lax.axis_index("seq")
@@ -276,6 +320,8 @@
     else:
         blocks, refs = refs[:len(ks)], refs[len(ks):]
         indices = [sender(me, k, g.peers) for k in ks]
+    if merged:
+        tails, refs = refs[:2], refs[2:]
     refs = refs if first else refs[1:]
     cache, refs = refs[0], refs[1:]
     if merged:
@@ -316,8 +362,13 @@
 
     each_page("start")
     if merged:
-        merge_partials([block.at[pl.ds(g.cap * length, tail_rows), :] for block in blocks],
-                       attended, *merged)
+        local, width, kj = merged
+        group = attended.shape[2] // width
+        for i, (value, _) in enumerate(merge_entries(tails, local, width, kj)):
+            value = value[:, 128 - width:].astype(jnp.bfloat16)
+            for row in range(kj):
+                k, j = row // group, row % group
+                attended[i, k:k + 1, j * width:(j + 1) * width] = value[row:row + 1]
     if g.full:
         for i, block in enumerate(blocks):
             rows = g.cap * (length + sum(size for _, size in passed))
@@ -327,10 +378,10 @@
         each_page("wait")
 
 
-def place(g, ks, labels, blocks, cache, pieces, passed=(), merged=None, shape=None):
+def place(g, ks, labels, blocks, cache, pieces, passed=(), merged=None, shape=None, tails=()):
     first = cache is None
     _, length = spread(pieces)
-    operands = [labels, *blocks] + ([] if first else [cache])
+    operands = [labels, *blocks, *tails] + ([] if first else [cache])
     outs = [jax.ShapeDtypeStruct((g.page_count, g.rows, 128), jnp.bfloat16)]
     out_specs = [HBM]
     if merged:
@@ -338,10 +389,9 @@
         out_specs.append(VMEM)
     number = g.peers if ks is None else len(ks)
     return pl.pallas_call(
-        functools.partial(place_kernel, g, ks, pieces, passed, first, merged,
-                          blocks[0].shape[-2] - g.cap * length),
+        functools.partial(place_kernel, g, ks, pieces, passed, first, merged),
         out_shape=outs,
-        in_specs=[SMEM] + [VMEM] * len(blocks) + [HBM] * (0 if first else 1),
+        in_specs=[SMEM] + [VMEM] * (len(blocks) + len(tails)) + [HBM] * (0 if first else 1),
         out_specs=out_specs,
         scratch_shapes=[pltpu.SemaphoreType.DMA((number,))],
         compiler_params=granted(2 * number * blocks[0].shape[-2] * 128),
@@ -414,42 +464,24 @@
         seq_total[s] = seq_total[s] + weights
         seq_sum[s] = seq_sum[s] + jnp.concatenate(sums, 0)
 
-    lane = lax.broadcasted_iota(jnp.int32, (kj, 128), 1)
-    diagonal = lane == lax.broadcasted_iota(jnp.int32, (kj, 128), 0)
-    shared = 128 // width
-
-    @pl.loop(0, g.peers)
+    @pl.loop(0, g.peers, unroll=4)
     def _(t):
-        lines = []
+        entries = []
         for i in range(local):
             s = t * local + i
             total = jnp.sum(seq_total[s], axis=1, keepdims=True)
             some = total > 0.0
             safe = jnp.where(some, total, 1.0)
             value = jnp.where(some, seq_sum[s] / safe, 0.0)
-            if i % shared:
-                value = pltpu.roll(value, 128 - width * (i % shared), 1)
-                value = jnp.where(lane < 128 - width * (i % shared), value, tile)
-            tile = value
-            if i % shared == shared - 1 or i == local - 1:
-                row = i // shared * kj
-                out[t, row:row + kj, :] = tile.astype(jnp.bfloat16)
             log = jnp.where(some, seq_max[s, :, :1] + jnp.log(safe), NEG_FILL)
-            log = jnp.broadcast_to(log, (kj, 128))
-            for _ in range(3):
-                part = log.astype(jnp.bfloat16).astype(jnp.float32)
-                log = log - part
-                lines.append(jnp.sum(jnp.where(diagonal, part, 0.0), axis=0, keepdims=True))
-        while len(lines) % 8:
-            lines.append(jnp.zeros((1, 128), jnp.float32))
-        parts = (local + shared - 1) // shared * kj
-        out[t, parts:parts + len(lines), :] = jnp.concatenate(lines, 0).astype(jnp.bfloat16)
+            entries.append((value, jnp.broadcast_to(log, (kj, 128))))
+        write_entries(out.at[t], entries, width)
 
 
 def attend(g, owner, fill, query, old, received, chunks, width, page_len):
     seqs, kj, _ = query.shape
     local = seqs // g.peers
-    extra = -(-local // (128 // width)) * kj + (3 * local + 7) // 8 * 8
+    extra = entry_rows(local, kj)
     blocks = [received[c][j] for j in range(g.groups - 1) for c in range(len(chunks))]
     return pl.pallas_call(
         functools.partial(attend_kernel, g, chunks, page_len, width, local),
@@ -499,7 +531,6 @@
     for c in range(1, len(SHARES) + 1):
         edges.append(max(rows * sum(SHARES[:c]) // sum(SHARES) // 8 * 8, edges[-1] + 8))
     chunks = tuple((a, b - a) for a, b in zip(edges, edges[1:]))
-    last = len(chunks) - 1
     old = old_cache.reshape(pages_own, all_heads * page_len, double)
 
     def swap(x, j):
@@ -530,10 +561,8 @@
     first_all = KINDS.index("all")
     pending = []
     for c, (kind, chunk) in enumerate(zip(KINDS, chunks)):
-        if c == last:
-            tail = attend(g, owner, fill, query, old, received, chunks, width, page_len)
         blocks = pack(g, None if kind == "all" else far, *pack_args, (chunk,),
-                      received[c:c + 1], tail, c == first_all, kind != "far")
+                      received[c:c + 1], None, c == first_all, kind != "far")
         if kind == "all":
             blocks = [lax.all_to_all(
                 blocks[0], "seq", split_axis=0, concat_axis=0, tiled=True)]
@@ -545,22 +574,30 @@
         if kind != "all":
             pending.append(c)
         if pending and kind != "fwd":
+            if kind == "far":
+                tail = attend(
+                    g, owner, fill, query, old, received, chunks, width, page_len)
             passed = tuple(i for i in pending if i in forwarded)
             blocks = pack(g, near, *pack_args, tuple(chunks[i] for i in pending),
-                          [received[i] for i in pending], single=False,
+                          [received[i] for i in pending], tail, single=False,
                           passed=tuple(chunks[i][1] for i in passed),
                           forwarded=[forwarded[i] for i in passed])
             blocks = route(blocks, near)
             incoming.append((near, blocks, tuple(chunks[i] for i in pending),
                              tuple(chunks[i] for i in passed)))
+            if tail is not None:
+                near_tails = (blocks, g.cap * sum(chunks[i][1] for i in pending))
             pending = []
     labels = read_labels(g, incoming[0][1][0], g.cap * chunks[first_all][1])
+    mine, across = reduce_near(*near_tails, seqs // peers, width, kj)
+    tails = [mine] + route([across], far[:1])
     cache = None
     for i, (ks, blocks, pieces, passed) in enumerate(incoming):
         merged = (seqs // peers, width, kj) if i == len(incoming) - 1 else None
         shape = (seqs // peers, heads, kj // heads * width)
         cache, *attended = place(
-            g, ks, labels, blocks, cache, pieces, passed, merged, shape)
+            g, ks, labels, blocks, cache, pieces, passed, merged, shape,
+            tails if merged else ())
     return cache.reshape(g.page_count, heads, page_len, double), attended[0]
 
 

time: 339 us -> 322 us (0.950)
  waiting for transfers between devices: 190 us -> 174 us
    ppermute x26 -> x27, waiting for transfers between devices: 111 us -> 79 us  [route(): lax.ppermute(block, 'seq', [(i, partner(i, k, peers)) for i in range(peer...]
    all_to_all x2, waiting for transfers between devices: 0.01 us -> 16.7 us  [per_device(): lax.all_to_all(blocks[0], 'seq', split_axis=0, concat_axis=0, tiled=True)]
    all_to_all x2, starting transfers between devices: 11.9 us -> 17.5 us  [per_device(): lax.all_to_all(blocks[0], 'seq', split_axis=0, concat_axis=0, tiled=True)]
    ppermute x26 -> x27, starting transfers between devices: 44.3 us -> 39 us  [route(): lax.ppermute(block, 'seq', [(i, partner(i, k, peers)) for i in range(peer...]
  transfers between devices with their start and end apart: 36 -> 37, of which waited for: 13 -> 14; matrix products, arithmetic and copies ran while one was open for 2% -> 3% of each run, Pallas kernels for 16% -> 17%
where the time goes in v1:
time: 322 us; the launch traced here: 321 us
  waiting for transfers between devices  174 us (54%)
  starting transfers between devices  66.8 us (21%)
  Pallas kernels  59.8 us (19%)
  local copies, waits for them, and re-layouts  18.6 us (6%)
    ppermute x27, waiting for transfers between devices, route(): lax.ppermute(block, 'seq', [(i, partner(i, k, peers)) for i in range(peer...  79 us
    ppermute x8, waiting for transfers between devices, swap(): lax.ppermute(x, 'head', [(i, (i + j) % groups) for i in range(groups)])  78.1 us
    ppermute x27, starting transfers between devices, route(): lax.ppermute(block, 'seq', [(i, partner(i, k, peers)) for i in range(peer...  39 us
    pallas_call x9, Pallas kernels, pack(): pl.pallas_call(functools.partial(pack_kernel, g, ks, single, pieces, pass...  29.6 us
    all_to_all x2, starting transfers between devices, per_device(): lax.all_to_all(blocks[0], 'seq', split_axis=0, concat_axis=0, tiled=True)  17.5 us
    all_to_all x2, waiting for transfers between devices, per_device(): lax.all_to_all(blocks[0], 'seq', split_axis=0, concat_axis=0, tiled=True)  16.7 us
    pallas_call x1, Pallas kernels, attend(): pl.pallas_call(functools.partial(attend_kernel, g, chunks, page_len, widt...  15.8 us
    dynamic_slice x7, local copies, waits for them, and re-layouts, per_device(): lax.dynamic_slice(source, (0, other * rows + start, 0), (pages_own, lengt...  11.8 us
  transfers between devices with their start and end apart: 37, of which 14 were waited for; matrix products, arithmetic and copies ran while one was open for 3% of the time, Pallas kernels for 17%

profile of v1, /device:TPU:0, one launch (start us, length us, event | category | flops | bytes accessed | tf_op | source)
XLA Modules:
  0.0 321.1 jit_solution(15816905214913446622)
XLA Ops:
  8.9 3.1 collective-permute-start.1
  12.0 23.2 %collective-permute-done.refs_1_ = s32[32]{0:T(128)S(1)} collective-permute-done((s32[32]{0:T(128)}, s32[32]{0:T(128)S(1)}, u32[]{:S(2)}, u32[]{:S(2)}) %collective-permute-start) | collective-permute-done | bytes 160 | tf_op jit(solution)/shard_map/ppermute | solution.py:537
  36.7 3.8 %pack.9 = bf16[16,520,128]{2,1,0:T(8,128)(2,1)} custom-call(s32[32]{0:T(128)} %refs_0_.17, s32[32]{0:T(128)} %copy-done.6, bf16[32,1024,128]{2,1,0:T(8,128)(2,1)} %bitcast.7, bf16[32,128,128]{2,1,0:T(8,128)(2,1)} %copy-done.3), custom_call_target="tpu_custom_call" | custom-call | flops 16777216 | bytes 4194304 | tf_op jit(solution)/shard_map/pack/pallas_call | solution.py:196
  40.5 6.1 %all-to-all-start = ((bf16[16,520,128]{2,1,0:T(8,128)(2,1)}), bf16[16,520,128]{2,1,0:T(8,128)(2,1)S(1)}, u32[]{:S(2)}, u32[]{:S(2)}) async-start(bf16[16,520,128]{2,1,0:T(8,128)(2,1)} %pack.9), calls=%async_computation | async-start | bytes 4259840 | tf_op jit(solution)/shard_map/all_to_all | solution.py:567
  51.9 15.5 %collective-permute-done.2.refs_3_.refs_10_ = bf16[32,80,128]{2,1,0:T(8,128)(2,1)S(1)} collective-permute-done((bf16[32,80,128]{2,1,0:T(8,128)(2,1)S(1)}, bf16[32,80,128]{2,1,0:T(8,128)(2,1)S(1)}, u32[]{:S(2)}, u32[]{:S(2)}) %collective-permute-start.2) | collective-permute-done | bytes 655392 | tf_op jit(solution)/shard_map/ppermute | solution.py:537
  68.3 3.3 %pack.10 = bf16[16,320,128]{2,1,0:T(8,128)(2,1)} custom-call(s32[32]{0:T(128)} %refs_0_.17, s32[32]{0:T(128)} %copy-done.6, bf16[32,1024,128]{2,1,0:T(8,128)(2,1)} %bitcast.10, bf16[32,80,128]{2,1,0:T(8,128)(2,1)} %copy-done.4), custom_call_target="tpu_custom_call" | custom-call | flops 10485760 | bytes 2621440 | tf_op jit(solution)/shard_map/pack/pallas_call | solution.py:196
  71.6 16.7 %all-to-all-done.blocks.refs_1_ = bf16[16,520,128]{2,1,0:T(8,128)(2,1)S(1)} async-done(((bf16[16,520,128]{2,1,0:T(8,128)(2,1)}), bf16[16,520,128]{2,1,0:T(8,128)(2,1)S(1)}, u32[]{:S(2)}, u32[]{:S(2)}) %all-to-all-start) | async-done | bytes 2129952 | tf_op jit(solution)/shard_map/all_to_all | solution.py:567
  88.2 11.3 %all-to-all-start.1 = ((bf16[16,320,128]{2,1,0:T(8,128)(2,1)}), bf16[16,320,128]{2,1,0:T(8,128)(2,1)S(1)}, u32[]{:S(2)}, u32[]{:S(2)}) async-start(bf16[16,320,128]{2,1,0:T(8,128)(2,1)} %pack.10), calls=%async_computation.1 | async-start | bytes 2621440 | tf_op jit(solution)/shard_map/all_to_all | solution.py:567
  109.1 39.4 %collective-permute-done.6.refs_6_.refs_3_.refs_5_ = bf16[32,48,128]{2,1,0:T(8,128)(2,1)} collective-permute-done((bf16[32,48,128]{2,1,0:T(8,128)(2,1)}, bf16[32,48,128]{2,1,0:T(8,128)(2,1)}, u32[]{:S(2)}, u32[]{:S(2)}) %collective-permute-start.6) | collective-permute-done | bytes 393248 | tf_op jit(solution)/shard_map/ppermute | solution.py:537
  151.1 2.8 collective-permute-start.26
  156.6 2.8 collective-permute-start.25
  165.0 2.8 collective-permute-start.24
  168.4 3.5 %pack.12 = (bf16[576,128]{1,0:T(8,128)(2,1)}, bf16[576,128]{1,0:T(8,128)(2,1)}, bf16[576,128]{1,0:T(8,128)(2,1)}, bf16[576,128]{1,0:T(8,128)(2,1)}, bf16[576,128...) custom-call(s32[32]{0:T(128)} %refs_0_.17, s32[32]{0:T(128)} %copy-done.6, ...), custom_call_target="tpu_custom_call" | custom-call | flops 9437184 | bytes 2359296 | tf_op jit(solution)/shard_map/pack/pallas_call | solution.py:196
  172.1 42.0 %collective-permute-done.24.refs_7_ = bf16[8,64,128]{2,1,0:T(8,128)(2,1)} collective-permute-done((bf16[8,64,128]{2,1,0:T(8,128)(2,1)}, bf16[8,64,128]{2,1,0:T(8,128)(2,1)}, u32[]{:S(2)}, u32[]{:S(2)}) %collective-permute-start.24) | collective-permute-done | bytes 131104 | tf_op jit(solution)/shard_map/ppermute | solution.py:542
  217.8 15.8 %attend.1.refs_4_ = bf16[16,72,128]{2,1,0:T(8,128)(2,1)} custom-call(s32[64]{0:T(128)} %copy-done.8, s32[64]{0:T(128)} %broadcast_select_fusion.refs_1_, bf16[32,32,128]{2,1,0:T(8,128)(2,1)} %pad.4.refs_2_, bf16[32,1024,128]{2,1,0:T(8,128)(2,1)} %bitcast.16, bf16[32,16,128]{2,1,0:T(8,128)(2,1)} %collective-permute-done.4.refs_4_.refs_3_, ...), custom_call_target="tpu_custom_call" | custom-call | flops 2147483648 | bytes 8388608 | tf_op jit(solution)/shard_map/attend/pallas_call | solution.py:486
  233.6 3.9 %pack.11 = (bf16[720,128]{1,0:T(8,128)(2,1)}, bf16[720,128]{1,0:T(8,128)(2,1)}, bf16[720,128]{1,0:T(8,128)(2,1)}, bf16[720,128]{1,0:T(8,128)(2,1)}, bf16[720,128...) custom-call(s32[32]{0:T(128)} %refs_0_.17, s32[32]{0:T(128)} %copy-done.6, ...), custom_call_target="tpu_custom_call" | custom-call | flops 9437184 | bytes 2359296 | tf_op jit(solution)/shard_map/pack/pallas_call | solution.py:196
  243.1 4.6 %pack.17 = (bf16[1280,128]{1,0:T(8,128)(2,1)}, bf16[1280,128]{1,0:T(8,128)(2,1)}, bf16[1280,128]{1,0:T(8,128)(2,1)}, bf16[1280,128]{1,0:T(8,128)(2,1)}, bf16[128...) custom-call(s32[32]{0:T(128)} %refs_0_.17, ...), custom_call_target="tpu_custom_call" | custom-call | flops 10485760 | bytes 2621440 | tf_op jit(solution)/shard_map/pack/pallas_call | solution.py:196
  251.0 4.2 %collective-permute-done.13.refs_6_.refs_7_ = bf16[720,128]{1,0:T(8,128)(2,1)} collective-permute-done((bf16[720,128]{1,0:T(8,128)(2,1)}, bf16[720,128]{1,0:T(8,128)(2,1)}, u32[]{:S(2)}, u32[]{:S(2)}) %collective-permute-start.13) | collective-permute-done | bytes 184352 | tf_op jit(solution)/shard_map/ppermute | solution.py:542
  261.4 8.3 %collective-permute-done.9.refs_2_.refs_3_ = bf16[720,128]{1,0:T(8,128)(2,1)S(1)} collective-permute-done((bf16[720,128]{1,0:T(8,128)(2,1)}, bf16[720,128]{1,0:T(8,128)(2,1)S(1)}, u32[]{:S(2)}, u32[]{:S(2)}) %collective-permute-start.9) | collective-permute-done | bytes 184352 | tf_op jit(solution)/shard_map/ppermute | solution.py:542
  273.2 3.3 %collective-permute-done.30.refs_4_ = bf16[1280,128]{1,0:T(8,128)(2,1)S(1)} collective-permute-done((bf16[1280,128]{1,0:T(8,128)(2,1)}, bf16[1280,128]{1,0:T(8,128)(2,1)S(1)}, u32[]{:S(2)}, u32[]{:S(2)}) %collective-permute-start.30) | collective-permute-done | bytes 327712 | tf_op jit(solution)/shard_map/ppermute | solution.py:542
  282.2 5.7 %collective-permute-done.33.refs_7_ = bf16[1280,128]{1,0:T(8,128)(2,1)S(1)} collective-permute-done((bf16[1280,128]{1,0:T(8,128)(2,1)}, bf16[1280,128]{1,0:T(8,128)(2,1)S(1)}, u32[]{:S(2)}, u32[]{:S(2)}) %collective-permute-start.33) | collective-permute-done | bytes 327712 | tf_op jit(solution)/shard_map/ppermute | solution.py:542
  291.3 6.6 %collective-permute-done.34.refs_8_ = bf16[1280,128]{1,0:T(8,128)(2,1)S(1)} collective-permute-done((bf16[1280,128]{1,0:T(8,128)(2,1)}, bf16[1280,128]{1,0:T(8,128)(2,1)S(1)}, u32[]{:S(2)}, u32[]{:S(2)}) %collective-permute-start.34) | collective-permute-done | bytes 327712 | tf_op jit(solution)/shard_map/ppermute | solution.py:542
  297.9 4.2 %collective-permute-start.15 = (bf16[72,128]{1,0:T(8,128)(2,1)S(1)}, bf16[72,128]{1,0:T(8,128)(2,1)S(1)}, u32[]{:S(2)}, u32[]{:S(2)}) collective-permute-start(bf16[72,128]{1,0:T(8,128)(2,1)S(1)} %get-tuple-element.65), channel_id=1, source_target_pairs={{0,16},{2,18},{4,20},{6,22},{8,24},{10,26},{12,28},{14,30},{16,0},... | collective-permute-start | bytes 55304 | tf_op jit(solution)/shard_map/ppermute | solution.py:542
  310.2 3.9 %collective-permute-done.23.refs_8_ = bf16[576,128]{1,0:T(8,128)(2,1)S(1)} collective-permute-done((bf16[576,128]{1,0:T(8,128)(2,1)}, bf16[576,128]{1,0:T(8,128)(2,1)S(1)}, u32[]{:S(2)}, u32[]{:S(2)}) %collective-permute-start.23) | collective-permute-done | bytes 147488 | tf_op jit(solution)/shard_map/ppermute | solution.py:542
  (105 shorter events, 83.0 us)
Async XLA Ops:
  8.9 26.3 %collective-permute-start.1 = (bf16[32,128,128]{2,1,0:T(8,128)(2,1)S(1)}, bf16[32,128,128]{2,1,0:T(8,128)(2,1)S(1)}, u32[]{:S(2)}, u32[]{:S(2)}) collective-permute-start(bf16[32,128,128]{2,1,0:T(8,128)(2,1)S(1)} %constant_dynamic-slice_fusion.2), channel_id=1, source_target_pairs={{0,1},{1,0},{2,3},{3,2},{4,5},{5,4},{6,7},{7,6},{8,9},{9,8},{10,11... | collective-permute-start | bytes 3145736 | tf_op jit(solution)/shard_map/ppermute | solution.py:537
  11.9 23.3 %collective-permute-start = (s32[32]{0:T(128)}, s32[32]{0:T(128)S(1)}, u32[]{:S(2)}, u32[]{:S(2)}) collective-permute-start(s32[32]{0:T(128)} %refs_0_.17), channel_id=1, source_target_pairs={{0,1},{1,0},{2,3},{3,2},{4,5},{5,4},{6,7},{7,6},{8,9},{9,8},{10,11... | collective-permute-start | bytes 392 | tf_op jit(solution)/shard_map/ppermute | solution.py:537
  40.5 47.7 %all-to-all-start = ((bf16[16,520,128]{2,1,0:T(8,128)(2,1)}), bf16[16,520,128]{2,1,0:T(8,128)(2,1)S(1)}, u32[]{:S(2)}, u32[]{:S(2)}) async-start(bf16[16,520,128]{2,1,0:T(8,128)(2,1)} %pack.9), calls=%async_computation | async-start | bytes 4259840 | tf_op jit(solution)/shard_map/all_to_all | solution.py:567
  88.2 230.3 %all-to-all-start.1 = ((bf16[16,320,128]{2,1,0:T(8,128)(2,1)}), bf16[16,320,128]{2,1,0:T(8,128)(2,1)S(1)}, u32[]{:S(2)}, u32[]{:S(2)}) async-start(bf16[16,320,128]{2,1,0:T(8,128)(2,1)} %pack.10), calls=%async_computation.1 | async-start | bytes 2621440 | tf_op jit(solution)/shard_map/all_to_all | solution.py:567
  99.6 68.8 %collective-permute-start.3 = (bf16[32,144,128]{2,1,0:T(8,128)(2,1)}, bf16[32,144,128]{2,1,0:T(8,128)(2,1)}, u32[]{:S(2)}, u32[]{:S(2)}) collective-permute-start(bf16[32,144,128]{2,1,0:T(8,128)(2,1)} %constant_dynamic-slice_fusion.1), channel_id=1, source_target_pairs={{0,1},{1,0},{2,3},{3,2},{4,5},{5,4},{6,7},{7,6},{8,9},{9,8},{10,11... | collective-permute-start | bytes 3538952 | tf_op jit(solution)/shard_map/ppermute | solution.py:537
  101.2 58.3 %collective-permute-start.7 = (bf16[32,64,128]{2,1,0:T(8,128)(2,1)}, bf16[32,64,128]{2,1,0:T(8,128)(2,1)}, u32[]{:S(2)}, u32[]{:S(2)}) collective-permute-start(bf16[32,64,128]{2,1,0:T(8,128)(2,1)} %constant_dynamic-slice_fusion.3), channel_id=1, source_target_pairs={{0,1},{1,0},{2,3},{3,2},{4,5},{5,4},{6,7},{7,6},{8,9},{9,8},{10,11... | collective-permute-start | bytes 1572872 | tf_op jit(solution)/shard_map/ppermute | solution.py:537
  101.7 46.8 %collective-permute-start.6 = (bf16[32,48,128]{2,1,0:T(8,128)(2,1)}, bf16[32,48,128]{2,1,0:T(8,128)(2,1)}, u32[]{:S(2)}, u32[]{:S(2)}) collective-permute-start(bf16[32,48,128]{2,1,0:T(8,128)(2,1)} %constant_dynamic-slice_fusion.4), channel_id=1, source_target_pairs={{0,1},{1,0},{2,3},{3,2},{4,5},{5,4},{6,7},{7,6},{8,9},{9,8},{10,11... | collective-permute-start | bytes 1179656 | tf_op jit(solution)/shard_map/ppermute | solution.py:537
  103.2 50.9 %collective-permute-start.5 = (bf16[32,32,128]{2,1,0:T(8,128)(2,1)}, bf16[32,32,128]{2,1,0:T(8,128)(2,1)}, u32[]{:S(2)}, u32[]{:S(2)}) collective-permute-start(bf16[32,32,128]{2,1,0:T(8,128)(2,1)} %constant_dynamic-slice_fusion.5), channel_id=1, source_target_pairs={{0,1},{1,0},{2,3},{3,2},{4,5},{5,4},{6,7},{7,6},{8,9},{9,8},{10,11... | collective-permute-start | bytes 786440 | tf_op jit(solution)/shard_map/ppermute | solution.py:537
  103.7 58.9 %collective-permute-start.4 = (bf16[32,16,128]{2,1,0:T(8,128)(2,1)}, bf16[32,16,128]{2,1,0:T(8,128)(2,1)}, u32[]{:S(2)}, u32[]{:S(2)}) collective-permute-start(bf16[32,16,128]{2,1,0:T(8,128)(2,1)} %constant_dynamic-slice_fusion.6), channel_id=1, source_target_pairs={{0,1},{1,0},{2,3},{3,2},{4,5},{5,4},{6,7},{7,6},{8,9},{9,8},{10,11... | collective-permute-start | bytes 393224 | tf_op jit(solution)/shard_map/ppermute | solution.py:537
  151.1 64.6 %collective-permute-start.26 = (bf16[8,192,128]{2,1,0:T(8,128)(2,1)}, bf16[8,192,128]{2,1,0:T(8,128)(2,1)}, u32[]{:S(2)}, u32[]{:S(2)}) collective-permute-start(bf16[8,192,128]{2,1,0:T(8,128)(2,1)} %pack.15), channel_id=1, source_target_pairs={{0,16},{2,18},{4,20},{6,22},{8,24},{10,26},{12,28},{14,30},{16,0},... | collective-permute-start | bytes 1179656 | tf_op jit(solution)/shard_map/ppermute | solution.py:542
  156.6 57.5 %collective-permute-start.25 = (bf16[8,128,128]{2,1,0:T(8,128)(2,1)}, bf16[8,128,128]{2,1,0:T(8,128)(2,1)}, u32[]{:S(2)}, u32[]{:S(2)}) collective-permute-start(bf16[8,128,128]{2,1,0:T(8,128)(2,1)} %pack.14), channel_id=1, source_target_pairs={{0,16},{2,18},{4,20},{6,22},{8,24},{10,26},{12,28},{14,30},{16,0},... | collective-permute-start | bytes 786440 | tf_op jit(solution)/shard_map/ppermute | solution.py:542
  162.3 75.3 %collective-permute-start.27 = (bf16[8,256,128]{2,1,0:T(8,128)(2,1)}, bf16[8,256,128]{2,1,0:T(8,128)(2,1)}, u32[]{:S(2)}, u32[]{:S(2)}) collective-permute-start(bf16[8,256,128]{2,1,0:T(8,128)(2,1)} %pack.16), channel_id=1, source_target_pairs={{0,16},{2,18},{4,20},{6,22},{8,24},{10,26},{12,28},{14,30},{16,0},... | collective-permute-start | bytes 1572872 | tf_op jit(solution)/shard_map/ppermute | solution.py:542
  165.0 49.1 %collective-permute-start.24 = (bf16[8,64,128]{2,1,0:T(8,128)(2,1)}, bf16[8,64,128]{2,1,0:T(8,128)(2,1)}, u32[]{:S(2)}, u32[]{:S(2)}) collective-permute-start(bf16[8,64,128]{2,1,0:T(8,128)(2,1)} %pack.13), channel_id=1, source_target_pairs={{0,16},{2,18},{4,20},{6,22},{8,24},{10,26},{12,28},{14,30},{16,0},... | collective-permute-start | bytes 393224 | tf_op jit(solution)/shard_map/ppermute | solution.py:542
  171.9 67.1 %collective-permute-start.16 = (bf16[576,128]{1,0:T(8,128)(2,1)}, bf16[576,128]{1,0:T(8,128)(2,1)}, u32[]{:S(2)}, u32[]{:S(2)}) collective-permute-start(bf16[576,128]{1,0:T(8,128)(2,1)} %get-tuple-element.66), channel_id=1, source_target_pairs={{0,16},{2,18},{4,20},{6,22},{8,24},{10,26},{12,28},{14,30},{16,0},... | collective-permute-start | bytes 442376 | tf_op jit(solution)/shard_map/ppermute | solution.py:542
  214.2 27.3 %collective-permute-start.17 = (bf16[576,128]{1,0:T(8,128)(2,1)}, bf16[576,128]{1,0:T(8,128)(2,1)}, u32[]{:S(2)}, u32[]{:S(2)}) collective-permute-start(bf16[576,128]{1,0:T(8,128)(2,1)} %get-tuple-element.67), channel_id=1, source_target_pairs={{0,18},{2,16},{4,22},{6,20},{8,26},{10,24},{12,30},{14,28},{16,2},... | collective-permute-start | bytes 442376 | tf_op jit(solution)/shard_map/ppermute | solution.py:542
  214.2 27.3 %collective-permute-start.18 = (bf16[576,128]{1,0:T(8,128)(2,1)}, bf16[576,128]{1,0:T(8,128)(2,1)}, u32[]{:S(2)}, u32[]{:S(2)}) collective-permute-start(bf16[576,128]{1,0:T(8,128)(2,1)} %get-tuple-element.68), channel_id=1, source_target_pairs={{0,20},{2,22},{4,16},{6,18},{8,28},{10,30},{12,24},{14,26},{16,4},... | collective-permute-start | bytes 442376 | tf_op jit(solution)/shard_map/ppermute | solution.py:542
  215.7 32.0 %collective-permute-start.19 = (bf16[576,128]{1,0:T(8,128)(2,1)}, bf16[576,128]{1,0:T(8,128)(2,1)}, u32[]{:S(2)}, u32[]{:S(2)}) collective-permute-start(bf16[576,128]{1,0:T(8,128)(2,1)} %get-tuple-element.69), channel_id=1, source_target_pairs={{0,22},{2,20},{4,18},{6,16},{8,30},{10,28},{12,26},{14,24},{16,6},... | collective-permute-start | bytes 442376 | tf_op jit(solution)/shard_map/ppermute | solution.py:542
  247.7 22.0 %collective-permute-start.28 = (bf16[1280,128]{1,0:T(8,128)(2,1)}, bf16[1280,128]{1,0:T(8,128)(2,1)S(1)}, u32[]{:S(2)}, u32[]{:S(2)}) collective-permute-start(bf16[1280,128]{1,0:T(8,128)(2,1)} %get-tuple-element.75), channel_id=1, source_target_pairs={{0,2},{2,0},{4,6},{6,4},{8,10},{10,8},{12,14},{14,12},{16,18},{18,... | collective-permute-start | bytes 983048 | tf_op jit(solution)/shard_map/ppermute | solution.py:542
  248.0 24.1 %collective-permute-start.29 = (bf16[1280,128]{1,0:T(8,128)(2,1)}, bf16[1280,128]{1,0:T(8,128)(2,1)S(1)}, u32[]{:S(2)}, u32[]{:S(2)}) collective-permute-start(bf16[1280,128]{1,0:T(8,128)(2,1)} %get-tuple-element.76), channel_id=1, source_target_pairs={{0,4},{2,6},{4,0},{6,2},{8,12},{10,14},{12,8},{14,10},{16,20},{18,... | collective-permute-start | bytes 983048 | tf_op jit(solution)/shard_map/ppermute | solution.py:542
  272.1 25.8 %collective-permute-start.34 = (bf16[1280,128]{1,0:T(8,128)(2,1)}, bf16[1280,128]{1,0:T(8,128)(2,1)S(1)}, u32[]{:S(2)}, u32[]{:S(2)}) collective-permute-start(bf16[1280,128]{1,0:T(8,128)(2,1)} %get-tuple-element.81), channel_id=1, source_target_pairs={{0,14},{2,12},{4,10},{6,8},{8,6},{10,4},{12,2},{14,0},{16,30},{18,... | collective-permute-start | bytes 983048 | tf_op jit(solution)/shard_map/ppermute | solution.py:542
  276.5 31.6 %collective-permute-start.20 = (bf16[576,128]{1,0:T(8,128)(2,1)}, bf16[576,128]{1,0:T(8,128)(2,1)S(1)}, u32[]{:S(2)}, u32[]{:S(2)}) collective-permute-start(bf16[576,128]{1,0:T(8,128)(2,1)} %get-tuple-element.70), channel_id=1, source_target_pairs={{0,24},{2,26},{4,28},{6,30},{8,16},{10,18},{12,20},{14,22},{16,8},... | collective-permute-start | bytes 442376 | tf_op jit(solution)/shard_map/ppermute | solution.py:542
  277.6 30.5 %collective-permute-start.21 = (bf16[576,128]{1,0:T(8,128)(2,1)}, bf16[576,128]{1,0:T(8,128)(2,1)S(1)}, u32[]{:S(2)}, u32[]{:S(2)}) collective-permute-start(bf16[576,128]{1,0:T(8,128)(2,1)} %get-tuple-element.71), channel_id=1, source_target_pairs={{0,26},{2,24},{4,30},{6,28},{8,18},{10,16},{12,22},{14,20},{16,10}... | collective-permute-start | bytes 442376 | tf_op jit(solution)/shard_map/ppermute | solution.py:542
  279.9 30.3 %collective-permute-start.22 = (bf16[576,128]{1,0:T(8,128)(2,1)}, bf16[576,128]{1,0:T(8,128)(2,1)S(1)}, u32[]{:S(2)}, u32[]{:S(2)}) collective-permute-start(bf16[576,128]{1,0:T(8,128)(2,1)} %get-tuple-element.72), channel_id=1, source_target_pairs={{0,28},{2,30},{4,24},{6,26},{8,20},{10,22},{12,16},{14,18},{16,12}... | collective-permute-start | bytes 442376 | tf_op jit(solution)/shard_map/ppermute | solution.py:542
  287.9 26.1 %collective-permute-start.23 = (bf16[576,128]{1,0:T(8,128)(2,1)}, bf16[576,128]{1,0:T(8,128)(2,1)S(1)}, u32[]{:S(2)}, u32[]{:S(2)}) collective-permute-start(bf16[576,128]{1,0:T(8,128)(2,1)} %get-tuple-element.73), channel_id=1, source_target_pairs={{0,30},{2,28},{4,26},{6,24},{8,22},{10,20},{12,18},{14,16},{16,14}... | collective-permute-start | bytes 442376 | tf_op jit(solution)/shard_map/ppermute | solution.py:542
  (24 other events, 454.1 us)
